TPU v7x, 32 devices: a whole 2x2x4 slice. The times are simulated.
32 devices in a mesh: expert: 4 (over z), shard: 8 (over y, x, core).
Axes of the slice: x: 2, y: 2, z: 4, core: 2. Of those that a mesh axis runs over, the one named last changes fastest.
Arguments:
- master_gate: float32 [64, 2048, 1408], P('expert', 'shard'), may hold values from -0.1875 to 0.1875
- master_up: float32 [64, 2048, 1408], P('expert', 'shard'), may hold values from -0.1875 to 0.1875
- router_weight: float32 [2048, 64], P('shard', 'expert'), may hold values from -0.125 to 0.125
- router_gain: float32 [2048], P('shard'), may hold values from 0.25 to 1.75
Outputs:
- final_gate: bfloat16 [64, 2048, 1408], P('expert', None, 'shard')
- final_up: bfloat16 [64, 2048, 1408], P('expert', None, 'shard')
- scale_gate: float32 [64, 1408], P('expert', 'shard')
- scale_up: float32 [64, 1408], P('expert', 'shard')
- serve_router: bfloat16 [2048, 64], replicated
All inputs are finite; a program needn't handle non-finite values.
Results may differ from a plain program's by a relative error of at most 0.001.
Values may be sent and summed in bfloat16 or wider, within the bound.
A program may use at most 192 MiB of HBM per device.

v0:
```python
import jax
import jax.numpy as jnp
from jax import lax
from jax.sharding import PartitionSpec as P


def local(master_gate, master_up, router_weight, router_gain):
    total_gate, total_up = lax.psum(
        (jnp.sum(master_gate * master_gate, axis=1), jnp.sum(master_up * master_up, axis=1)),
        "shard",
    )
    scale_gate = jnp.sqrt(total_gate)
    scale_up = jnp.sqrt(total_up)
    narrow_gate, narrow_up = (
        (master_gate / jnp.expand_dims(scale_gate, 1)).astype(jnp.bfloat16),
        (master_up / jnp.expand_dims(scale_up, 1)).astype(jnp.bfloat16),
    )
    final_gate, final_up = (
        lax.all_to_all(narrow_gate, "shard", split_axis=2, concat_axis=1, tiled=True),
        lax.all_to_all(narrow_up, "shard", split_axis=2, concat_axis=1, tiled=True),
    )
    scale_gate = lax.dynamic_slice_in_dim(
        scale_gate, lax.axis_index("shard") * final_gate.shape[2], final_gate.shape[2], axis=1
    )
    scale_up = lax.dynamic_slice_in_dim(
        scale_up, lax.axis_index("shard") * final_up.shape[2], final_up.shape[2], axis=1
    )
    part_router = (router_weight * router_gain[:, None]).astype(jnp.bfloat16)
    row_router = lax.all_gather(part_router, "shard", axis=0, tiled=True)
    serve_router = lax.all_gather(row_router, "expert", axis=1, tiled=True)
    return (final_gate, final_up, scale_gate, scale_up, serve_router)


def solution(mesh):
    in_specs = (
        P("expert", "shard", None),
        P("expert", "shard", None),
        P("shard", "expert"),
        P("shard"),
    )
    out_specs = (
        P("expert", None, "shard"),
        P("expert", None, "shard"),
        P("expert", "shard"),
        P("expert", "shard"),
        P(),
    )
    return jax.shard_map(local, mesh=mesh, in_specs=in_specs, out_specs=out_specs, check_vma=False)
```

profile of v0, /device:TPU:0, one launch (start us, length us, event | category | flops | bytes accessed | tf_op | source)
XLA Modules:
  0.0 445.2 jit_solution(13781813590717320649)
XLA Ops:
  7.2 0.0 all-reduce.3.cloned.1.call-start
  7.2 15.8 %multiply_reduce_fusion = (f32[16,1408]{1,0:T(8,128)}, f32[16,1408]{1,0:T(8,128)}) fusion(f32[16,256,1408]{2,1,0:T(8,128)} %param.5, f32[16,256,1408]{2,1,0:T(8,128)} %param.4), kind=kLoop, calls=%fused_computation.1 | loop fusion | flops 23023616 | bytes 46317568 | tf_op jit(solution)/shard_map/reduce_sum | solution.py:9
  23.0 0.0 all-reduce.3.cloned.1.call-update
  23.1 23.7 %copy.22 = f32[16,256,1408]{1,0,2:T(8,128)} copy(f32[16,256,1408]{2,1,0:T(8,128)} %param.5) | data formatting | bytes 46137344 | tf_op args[1]
  46.8 32.3 %all-reduce.3.cloned.1.call-done = (f32[16,1408]{1,0:T(8,128)}, f32[16,1408]{1,0:T(8,128)}) async-done(((f32[16,1408]{1,0:T(8,128)}, f32[16,1408]{1,0:T(8,128)}), (f32[16,1408]{1,0:T(8,128)}, f32[16,1408]{1,0:T(8,128)})) %all-reduce.3.cloned.1.call-update) | async-done | bytes 180240 | tf_op jit(solution)/shard_map/psum | solution.py:8
  79.0 0.9 sqrt.7
  80.0 0.3 copy.21
  80.2 14.2 %divide_convert_fusion = bf16[16,256,1408]{1,0,2:T(8,128)(2,1)} fusion(f32[16,256,1408]{1,0,2:T(8,128)} %copy.22, f32[16,1408]{0,1:T(8,128)S(1)} %copy.21), kind=kLoop, calls=%fused_computation | loop fusion | flops 11534336 | bytes 34693120 | tf_op jit(solution)/shard_map/convert_element_type | solution.py:16
  94.4 5.2 %all-to-all-start.1 = ((bf16[16,256,1408]{1,0,2:T(8,128)(2,1)}), bf16[16,256,1408]{1,0,2:T(8,128)(2,1)}, u32[]{:S(2)}, u32[]{:S(2)}) async-start(bf16[16,256,1408]{1,0,2:T(8,128)(2,1)} %divide_convert_fusion), calls=%async_computation.1 | async-start | bytes 23068672 | tf_op jit(solution)/shard_map/all_to_all | solution.py:20
  99.7 0.0 copy-start
  99.7 23.7 %copy.18 = f32[16,256,1408]{1,0,2:T(8,128)} copy(f32[16,256,1408]{2,1,0:T(8,128)} %param.4) | data formatting | bytes 46137344 | tf_op args[0]
  123.4 0.0 copy-done
  123.4 0.3 copy.17
  123.7 0.0 copy-start.1
  123.7 0.0 copy-start.2
  123.7 14.2 %divide_convert_fusion.1 = bf16[16,256,1408]{1,0,2:T(8,128)(2,1)} fusion(f32[16,256,1408]{1,0,2:T(8,128)} %copy.18, f32[16,1408]{0,1:T(8,128)S(1)} %copy.17), kind=kLoop, calls=%fused_computation.2 | loop fusion | flops 11534336 | bytes 34693120 | tf_op jit(solution)/shard_map/convert_element_type | solution.py:15
  138.0 89.5 %all-to-all-done.1 = bf16[16,256,1408]{1,0,2:T(8,128)(2,1)} async-done(((bf16[16,256,1408]{1,0,2:T(8,128)(2,1)}), bf16[16,256,1408]{1,0,2:T(8,128)(2,1)}, u32[]{:S(2)}, u32[]{:S(2)}) %all-to-all-start.1) | async-done | bytes 11534368 | tf_op jit(solution)/shard_map/all_to_all | solution.py:20
  227.4 5.3 %all-to-all-start = ((bf16[16,256,1408]{1,0,2:T(8,128)(2,1)}), bf16[16,256,1408]{1,0,2:T(8,128)(2,1)}, u32[]{:S(2)}, u32[]{:S(2)}) async-start(bf16[16,256,1408]{1,0,2:T(8,128)(2,1)} %divide_convert_fusion.1), calls=%async_computation | async-start | bytes 23068672 | tf_op jit(solution)/shard_map/all_to_all | solution.py:19
  232.7 0.0 copy-done.1
  232.7 0.0 copy-done.2
  232.7 130.9 %all_gather.6 = bf16[2048,16]{0,1:T(8,128)(2,1)S(1)} all-gather(bf16[256,16]{0,1:T(8,128)(2,1)S(1)} %multiply_convert_fusion), channel_id=1, replica_groups=mesh['expert'=4,'shard'=8] {'shard'}, dimensions={0}, use_global_device_ids=true | all-gather | bytes 73728 | tf_op jit(solution)/shard_map/all_gather | solution.py:29
  363.6 14.0 %all_gather.7 = bf16[2048,64]{0,1:T(8,128)(2,1)S(1)} all-gather(bf16[2048,16]{0,1:T(8,128)(2,1)S(1)} %all_gather.6), channel_id=1, replica_groups=mesh['expert'=4,'shard'=8] {'expert'}, dimensions={1}, use_global_device_ids=true | all-gather | bytes 327680 | tf_op jit(solution)/shard_map/all_gather | solution.py:30
  377.6 0.7 constant_dynamic-slice_fusion
  378.3 0.7 constant_dynamic-slice_fusion.1
  379.0 11.4 %copy.24 = bf16[16,8,256,176]{2,1,3,0:T(8,128)(2,1)} copy(bf16[16,8,256,176]{2,0,3,1:T(8,128)(2,1)} %bitcast.5) | data formatting | bytes 23068672 | tf_op jit(solution)/shard_map/all_to_all | solution.py:20
  390.4 18.0 %all_to_all.33 = bf16[16,2048,176]{1,2,0:T(8,128)(2,1)} reshape(bf16[16,8,256,176]{2,1,3,0:T(8,128)(2,1)} %copy.24) | data formatting | bytes 23068672 | tf_op jit(solution)/shard_map/all_to_all | solution.py:20
  408.3 0.0 all-to-all-done
  408.3 11.4 %copy.20 = bf16[16,8,256,176]{2,1,3,0:T(8,128)(2,1)} copy(bf16[16,8,256,176]{2,0,3,1:T(8,128)(2,1)} %bitcast.2) | data formatting | bytes 23068672 | tf_op jit(solution)/shard_map/all_to_all | solution.py:19
  419.7 18.0 %all_to_all.29 = bf16[16,2048,176]{1,2,0:T(8,128)(2,1)} reshape(bf16[16,8,256,176]{2,1,3,0:T(8,128)(2,1)} %copy.20) | data formatting | bytes 23068672 | tf_op jit(solution)/shard_map/all_to_all | solution.py:19
  437.7 0.7 copy.30
  (2 shorter events, 0.0 us)
Async XLA Ops:
  7.2 71.9 %all-reduce.3.cloned.1.call-start = ((), (), s32[]{:S(2)}) async-start(), calls=%async_computation.2 | async-start | bytes 360448 | tf_op jit(solution)/shard_map/psum | solution.py:8
  94.4 133.0 %all-to-all-start.1 = ((bf16[16,256,1408]{1,0,2:T(8,128)(2,1)}), bf16[16,256,1408]{1,0,2:T(8,128)(2,1)}, u32[]{:S(2)}, u32[]{:S(2)}) async-start(bf16[16,256,1408]{1,0,2:T(8,128)(2,1)} %divide_convert_fusion), calls=%async_computation.1 | async-start | bytes 23068672 | tf_op jit(solution)/shard_map/all_to_all | solution.py:20
  99.7 23.7 %copy-start = (f32[16,1408]{1,0:T(8,128)S(1)}, f32[16,1408]{1,0:T(8,128)}, u32[]{:S(2)}) copy-start(f32[16,1408]{1,0:T(8,128)} %get-tuple-element.5) | copy-start | bytes 270340
  123.7 109.0 %copy-start.1 = (f32[256,16]{0,1:T(8,128)S(1)}, f32[256,16]{0,1:T(8,128)}, u32[]{:S(2)}) copy-start(f32[256,16]{0,1:T(8,128)} %param.6) | copy-start | bytes 49156
  123.7 109.0 %copy-start.2 = (f32[256]{0:T(256)S(1)}, f32[256]{0:T(256)}, u32[]{:S(2)}) copy-start(f32[256]{0:T(256)} %param.7) | copy-start | bytes 3076
  227.4 180.9 %all-to-all-start = ((bf16[16,256,1408]{1,0,2:T(8,128)(2,1)}), bf16[16,256,1408]{1,0,2:T(8,128)(2,1)}, u32[]{:S(2)}, u32[]{:S(2)}) async-start(bf16[16,256,1408]{1,0,2:T(8,128)(2,1)} %divide_convert_fusion.1), calls=%async_computation | async-start | bytes 23068672 | tf_op jit(solution)/shard_map/all_to_all | solution.py:19
Sparse Core Ops, SparseCore 0:
  23.2 55.8 all-reduce.2
where the time goes:
time: 447 us; the launch traced here: 445 us
  blocking collectives  145 us (32%)
  waiting for transfers between devices  122 us (27%)
  local copies, waits for them, and re-layouts  110 us (25%)
  other arithmetic  44.3 us (10%)
  between operations  14.1 us (3%)
  starting transfers between devices  10.5 us (2%)
    all_gather x1, blocking collectives, local(): row_router = lax.all_gather(part_router, 'shard', axis=0, tiled=True)  131 us
    all_to_all x1, waiting for transfers between devices, local(): lax.all_to_all(narrow_up, 'shard', split_axis=2, concat_axis=1, tiled=True)  89.5 us
    unnamed x9, local copies, waits for them, and re-layouts  48.1 us
    psum x1, waiting for transfers between devices, local(): lax.psum((jnp.sum(master_gate * master_gate, axis=1), jnp.sum(master_up *...  32.3 us
    all_to_all x2, local copies, waits for them, and re-layouts, local(): lax.all_to_all(narrow_gate, 'shard', split_axis=2, concat_axis=1, tiled=T...  29.3 us
    all_to_all x2, local copies, waits for them, and re-layouts, local(): lax.all_to_all(narrow_up, 'shard', split_axis=2, concat_axis=1, tiled=True)  29.3 us
    reduce_sum x1, other arithmetic, local(): jnp.sum(master_up * master_up, axis=1)  15.8 us
    convert_element_type x1, other arithmetic, local(): (master_up / jnp.expand_dims(scale_up, 1)).astype(jnp.bfloat16)  14.2 us
  transfers between devices with their start and end apart: 3, of which 2 were waited for; matrix products, arithmetic and copies ran while one was open for 17% of the time, Pallas kernels for 0%

commit v1 on v0

--- a/solution.py
+++ b/solution.py
@@ -2,6 +2,12 @@
 import jax.numpy as jnp
 from jax import lax
 from jax.sharding import PartitionSpec as P
+
+
+def stacked_exchange(array, mesh_axis, split, join):
+    pieces = jnp.split(array, lax.axis_size(mesh_axis), axis=split)
+    received = lax.all_to_all(jnp.stack(pieces), mesh_axis, 0, 0)
+    return jnp.concatenate(received, axis=join)
 
 
 def local(master_gate, master_up, router_weight, router_gain):
@@ -17,7 +23,7 @@
     )
     final_gate, final_up = (
         lax.all_to_all(narrow_gate, "shard", split_axis=2, concat_axis=1, tiled=True),
-        lax.all_to_all(narrow_up, "shard", split_axis=2, concat_axis=1, tiled=True),
+        stacked_exchange(narrow_up, "shard", 2, 1),
     )
     scale_gate = lax.dynamic_slice_in_dim(
         scale_gate, lax.axis_index("shard") * final_gate.shape[2], final_gate.shape[2], axis=1

time: 447 us -> 428 us (0.957)
  local copies, waits for them, and re-layouts: 110 us -> 99.3 us
  waiting for transfers between devices: 122 us -> 117 us
    all_to_all x1, waiting for transfers between devices: 89.5 us -> 0.01 us  [stacked_exchange(): received = lax.all_to_all(jnp.stack(pieces), mesh_axis, 0, 0)]
    all_to_all x1, waiting for transfers between devices: 0.01 us -> 84.8 us  [local(): lax.all_to_all(narrow_gate, 'shard', split_axis=2, concat_axis=1, tiled=T...]
    all_to_all x2 -> x0, local copies, waits for them, and re-layouts: 29.3 us -> none  [local(): lax.all_to_all(narrow_up, 'shard', split_axis=2, concat_axis=1, tiled=True)]
    reshape x0 -> x1, local copies, waits for them, and re-layouts: none -> 10 us  [stacked_exchange(): return jnp.concatenate(received, axis=join)]
    unnamed x9 -> x16, local copies, waits for them, and re-layouts: 48.1 us -> 56.2 us
  transfers between devices with their start and end apart: 3 -> 3, of which waited for: 2 -> 2; matrix products, arithmetic and copies ran while one was open for 17% -> 19% of each run, Pallas kernels for 0% -> 0%
where the time goes in v1:
time: 428 us; the launch traced here: 426 us
  blocking collectives  145 us (34%)
  waiting for transfers between devices  117 us (27%)
  local copies, waits for them, and re-layouts  99.3 us (23%)
  other arithmetic  39.9 us (9%)
  between operations  14.1 us (3%)
  starting transfers between devices  10.5 us (2%)
    all_gather x1, blocking collectives, local(): row_router = lax.all_gather(part_router, 'shard', axis=0, tiled=True)  131 us
    all_to_all x1, waiting for transfers between devices, local(): lax.all_to_all(narrow_gate, 'shard', split_axis=2, concat_axis=1, tiled=T...  84.8 us
    unnamed x16, local copies, waits for them, and re-layouts  56.2 us
    psum x1, waiting for transfers between devices, local(): lax.psum((jnp.sum(master_gate * master_gate, axis=1), jnp.sum(master_up *...  32.3 us
    all_to_all x2, local copies, waits for them, and re-layouts, local(): lax.all_to_all(narrow_gate, 'shard', split_axis=2, concat_axis=1, tiled=T...  29.3 us
    reduce_sum x1, other arithmetic, local(): jnp.sum(master_up * master_up, axis=1)  15.8 us
    convert_element_type x1, other arithmetic, local(): (master_gate / jnp.expand_dims(scale_gate, 1)).astype(jnp.bfloat16)  14.2 us
    all_gather x1, blocking collectives, local(): serve_router = lax.all_gather(row_router, 'expert', axis=1, tiled=True)  14 us
  transfers between devices with their start and end apart: 3, of which 2 were waited for; matrix products, arithmetic and copies ran while one was open for 19% of the time, Pallas kernels for 0%

profile of v1, /device:TPU:0, one launch (start us, length us, event | category | flops | bytes accessed | tf_op | source)
XLA Modules:
  0.0 425.9 jit_solution(538050658232664243)
XLA Ops:
  7.2 0.0 all-reduce.3.cloned.1.call-start
  7.2 15.8 %multiply_reduce_fusion = (f32[16,1408]{1,0:T(8,128)}, f32[16,1408]{1,0:T(8,128)}) fusion(f32[16,256,1408]{2,1,0:T(8,128)} %param.5, f32[16,256,1408]{2,1,0:T(8,128)} %param.4), kind=kLoop, calls=%fused_computation.1 | loop fusion | flops 23023616 | bytes 46317568 | tf_op jit(solution)/shard_map/reduce_sum | solution.py:15
  23.0 0.0 all-reduce.3.cloned.1.call-update
  23.1 23.7 %copy.22 = f32[16,256,1408]{1,0,2:T(8,128)} copy(f32[16,256,1408]{2,1,0:T(8,128)} %param.4) | data formatting | bytes 46137344 | tf_op args[0]
  46.8 32.3 %all-reduce.3.cloned.1.call-done = (f32[16,1408]{1,0:T(8,128)}, f32[16,1408]{1,0:T(8,128)}) async-done(((f32[16,1408]{1,0:T(8,128)}, f32[16,1408]{1,0:T(8,128)}), (f32[16,1408]{1,0:T(8,128)}, f32[16,1408]{1,0:T(8,128)})) %all-reduce.3.cloned.1.call-update) | async-done | bytes 180240 | tf_op jit(solution)/shard_map/psum | solution.py:14
  79.0 0.9 sqrt.6
  80.0 0.3 copy.21
  80.2 14.2 %divide_convert_fusion.1 = bf16[16,256,1408]{1,0,2:T(8,128)(2,1)} fusion(f32[16,256,1408]{1,0,2:T(8,128)} %copy.22, f32[16,1408]{0,1:T(8,128)S(1)} %copy.21), kind=kLoop, calls=%fused_computation.2 | loop fusion | flops 11534336 | bytes 34693120 | tf_op jit(solution)/shard_map/convert_element_type | solution.py:21
  94.4 5.2 %all-to-all-start = ((bf16[16,256,1408]{1,0,2:T(8,128)(2,1)}), bf16[16,256,1408]{1,0,2:T(8,128)(2,1)}, u32[]{:S(2)}, u32[]{:S(2)}) async-start(bf16[16,256,1408]{1,0,2:T(8,128)(2,1)} %divide_convert_fusion.1), calls=%async_computation | async-start | bytes 23068672 | tf_op jit(solution)/shard_map/all_to_all | solution.py:25
  99.7 0.0 copy-start
  99.7 23.4 %copy.25 = f32[16,256,1408]{1,2,0:T(8,128)} copy(f32[16,256,1408]{2,1,0:T(8,128)} %param.5) | data formatting | bytes 46137344 | tf_op args[1]
  123.1 0.0 copy-done
  123.1 9.8 %divide_convert_fusion = bf16[16,256,1408]{1,2,0:T(8,128)(2,1)S(1)} fusion(f32[16,256,1408]{1,2,0:T(8,128)} %copy.25, f32[16,1408]{1,0:T(8,128)S(1)} %sqrt.7), kind=kLoop, calls=%fused_computation | loop fusion | flops 11534336 | bytes 34693120 | tf_op jit(solution)/shard_map/convert_element_type | solution.py:22
  132.9 1.2 fusion.7
  134.1 1.2 fusion.6
  135.4 1.2 fusion.5
  136.6 1.2 fusion.4
  137.8 1.2 fusion.3
  139.0 1.2 fusion.2
  140.2 1.2 fusion.1
  141.4 1.2 fusion
  142.6 0.0 copy-start.1
  142.6 0.0 copy-start.2
  142.6 84.8 %all-to-all-done = bf16[16,256,1408]{1,0,2:T(8,128)(2,1)} async-done(((bf16[16,256,1408]{1,0,2:T(8,128)(2,1)}), bf16[16,256,1408]{1,0,2:T(8,128)(2,1)}, u32[]{:S(2)}, u32[]{:S(2)}) %all-to-all-start) | async-done | bytes 11534368 | tf_op jit(solution)/shard_map/all_to_all | solution.py:25
  227.4 5.3 %all-to-all-start.1 = ((bf16[8,16,256,176]{2,3,1,0:T(8,128)(2,1)}), bf16[8,16,256,176]{2,3,1,0:T(8,128)(2,1)}, u32[]{:S(2)}, u32[]{:S(2)}) async-start(bf16[8,16,256,176]{2,3,1,0:T(8,128)(2,1)} %fusion), calls=%async_computation.1 | async-start | bytes 23068672 | tf_op jit(solution)/shard_map/all_to_all | solution.py:9
  232.7 0.0 copy-done.1
  232.7 0.0 copy-done.2
  232.7 130.9 %all_gather.6 = bf16[2048,16]{0,1:T(8,128)(2,1)S(1)} all-gather(bf16[256,16]{0,1:T(8,128)(2,1)S(1)} %multiply_convert_fusion), channel_id=1, replica_groups=mesh['expert'=4,'shard'=8] {'shard'}, dimensions={0}, use_global_device_ids=true | all-gather | bytes 73728 | tf_op jit(solution)/shard_map/all_gather | solution.py:35
  363.6 14.0 %all_gather.7 = bf16[2048,64]{0,1:T(8,128)(2,1)S(1)} all-gather(bf16[2048,16]{0,1:T(8,128)(2,1)S(1)} %all_gather.6), channel_id=1, replica_groups=mesh['expert'=4,'shard'=8] {'expert'}, dimensions={1}, use_global_device_ids=true | all-gather | bytes 327680 | tf_op jit(solution)/shard_map/all_gather | solution.py:36
  377.6 0.7 constant_dynamic-slice_fusion.1
  378.3 0.7 constant_dynamic-slice_fusion
  379.0 11.3 %copy.24 = bf16[16,8,256,176]{2,1,3,0:T(8,128)(2,1)} copy(bf16[16,8,256,176]{2,0,3,1:T(8,128)(2,1)} %bitcast.2) | data formatting | bytes 23068672 | tf_op jit(solution)/shard_map/all_to_all | solution.py:25
  390.3 18.0 %all_to_all.19 = bf16[16,2048,176]{1,2,0:T(8,128)(2,1)} reshape(bf16[16,8,256,176]{2,1,3,0:T(8,128)(2,1)} %copy.24) | data formatting | bytes 23068672 | tf_op jit(solution)/shard_map/all_to_all | solution.py:25
  408.3 0.0 all-to-all-done.1
  408.3 10.0 %copy.28 = bf16[8,16,22,8,256]{4,3,0,2,1:T(8,128)(2,1)} copy(bf16[8,16,22,8,256]{4,3,2,1,0:T(8,128)(2,1)} %bitcast.12) | data formatting | bytes 23068672 | tf_op jit(solution)/shard_map/reshape | solution.py:10
  418.3 0.7 copy.39
  (2 shorter events, 0.0 us)
Async XLA Ops:
  7.2 71.9 %all-reduce.3.cloned.1.call-start = ((), (), s32[]{:S(2)}) async-start(), calls=%async_computation.2 | async-start | bytes 360448 | tf_op jit(solution)/shard_map/psum | solution.py:14
  94.4 133.0 %all-to-all-start = ((bf16[16,256,1408]{1,0,2:T(8,128)(2,1)}), bf16[16,256,1408]{1,0,2:T(8,128)(2,1)}, u32[]{:S(2)}, u32[]{:S(2)}) async-start(bf16[16,256,1408]{1,0,2:T(8,128)(2,1)} %divide_convert_fusion.1), calls=%async_computation | async-start | bytes 23068672 | tf_op jit(solution)/shard_map/all_to_all | solution.py:25
  99.7 23.4 %copy-start = (f32[16,1408]{1,0:T(8,128)S(1)}, f32[16,1408]{1,0:T(8,128)}, u32[]{:S(2)}) copy-start(f32[16,1408]{1,0:T(8,128)} %get-tuple-element.6) | copy-start | bytes 270340
  142.6 90.1 %copy-start.1 = (f32[256,16]{0,1:T(8,128)S(1)}, f32[256,16]{0,1:T(8,128)}, u32[]{:S(2)}) copy-start(f32[256,16]{0,1:T(8,128)} %param.6) | copy-start | bytes 49156
  142.6 90.1 %copy-start.2 = (f32[256]{0:T(256)S(1)}, f32[256]{0:T(256)}, u32[]{:S(2)}) copy-start(f32[256]{0:T(256)} %param.7) | copy-start | bytes 3076
  227.4 180.9 %all-to-all-start.1 = ((bf16[8,16,256,176]{2,3,1,0:T(8,128)(2,1)}), bf16[8,16,256,176]{2,3,1,0:T(8,128)(2,1)}, u32[]{:S(2)}, u32[]{:S(2)}) async-start(bf16[8,16,256,176]{2,3,1,0:T(8,128)(2,1)} %fusion), calls=%async_computation.1 | async-start | bytes 23068672 | tf_op jit(solution)/shard_map/all_to_all | solution.py:9
Sparse Core Ops, SparseCore 0:
  23.2 55.8 all-reduce.2
